TPU v7x, 32 devices: a whole 2x2x4 slice. The times are simulated.
32 devices in a mesh: groups: 2 (over y), dp: 4 (over z), section: 2 (over x), tensor: 2 (over core).
Axes of the slice: x: 2, y: 2, z: 4, core: 2. Of those that a mesh axis runs over, the one named last changes fastest.
Arguments:
- hidden: bfloat16 [128, 8, 5120], P(('groups', 'dp')), parts along dimension 0, may hold values from -6 to 6
- unembed: bfloat16 [128, 8, 5120], P(('groups', 'dp')), parts along dimension 0, may hold values from -0.02734375 to 0.02734375
- value_proj: bfloat16 [2, 5120, 512], P('section', 'dp', 'tensor'), may hold values from -0.078125 to 0.078125
- output_proj: bfloat16 [2, 512, 5120], P('section', 'tensor', 'dp'), may hold values from -0.125 to 0.125
- norm_gains: float32 [2, 5120], P('section'), may hold values from 0.1 to 1.9
- survive: int32 [8], P(('groups', 'dp')), parts along dimension 0, may hold values from 0 to 1, as said below
- lengths: int32 [128], P(('groups', 'dp')), parts along dimension 0, may hold values from 1 to 8
- assign: int32 [128], P(('groups', 'dp')), parts along dimension 0, may hold values from 0 to 16, as said below
- advantage: float32 [128], P(('groups', 'dp')), parts along dimension 0, may hold values from -4 to 4
- reference_logit: float32 [128, 8], P(('groups', 'dp')), parts along dimension 0, may hold values from -4 to 4
- recorded_gap: float32 [128, 8], P(('groups', 'dp')), parts along dimension 0, may hold values from -2 to 2
Outputs:
- grad_value: float32 [4, 5120, 512], P(('groups', 'section'), 'dp', 'tensor'), parts along dimension 0
- grad_output: float32 [4, 512, 5120], P(('groups', 'section'), 'tensor', 'dp'), parts along dimension 0
There are 2 independent parts, one for each index of `groups`. A program takes and returns all parts, laid end to end along the dimension named above; an argument that names none is the same for every part. Nothing has to cross between parts.
Inputs may be any that keep to these rules, and one draw needn't show every extreme that they name: `survive`: 1 where the group of 16 responses is kept, 0 where it is dropped; in every draw all groups of some dp index are kept. `assign`: the 16 slots of a dp index list the local positions (0 to 15) of the responses of its kept groups, each exactly once, then hold 16 in every other slot.
All inputs are finite; a program needn't handle non-finite values.
Results may differ from a plain program's by a relative error of at most 0.029.
Values may be sent and summed in bfloat16 or wider, within the bound.
A program may use at most 64 MiB of HBM per device.

v0:
```python
import math
import jax
import jax.numpy as jnp
from jax import lax
from jax.sharding import PartitionSpec as P

GROUP = 16
MB_RESP = 8
eps_norm = 1e-06
loss_scale = 4096.0
clip_high = math.log(1.28)
clip_low = math.log(0.8)


def from_behind(block, axis, distance):
    devices = range(lax.axis_size(axis))
    route = [(i - distance, i) for i in devices if i - distance in devices]
    return lax.ppermute(block, axis, route)


def norm_forward(row_block, norm_gain):
    values = row_block.astype(jnp.float32)
    inverse = lax.rsqrt(jnp.mean(values * values, axis=-1, keepdims=True) + eps_norm)
    return (values, inverse, (values * inverse * norm_gain).astype(jnp.bfloat16))


def norm_backward(values, inverse, norm_gain, upstream):
    scaled = upstream * norm_gain
    inner_sum = jnp.sum(scaled * values, axis=-1, keepdims=True) / values.shape[-1]
    return inverse * scaled - values * (inverse * inverse * inverse) * inner_sum


def contract_last(left_rows, right_rows):
    return lax.dot_general(
        left_rows, right_rows, (((1,), (1,)), ((), ())), preferred_element_type=jnp.float32
    )


def contract_first(left_rows, right_rows):
    return lax.dot_general(
        left_rows, right_rows, (((0,), (0,)), ((), ())), preferred_element_type=jnp.float32
    )


def take_slot(slot_store, slot_index):
    return lax.dynamic_index_in_dim(slot_store, slot_index, 0, keepdims=False)


def put_slot(slot_store, new_value, slot_index, active):
    previous = take_slot(slot_store, slot_index)
    return lax.dynamic_update_index_in_dim(
        slot_store, jnp.where(active, new_value, previous), slot_index, 0
    )


def local(
    hidden,
    unembed,
    value_proj,
    output_proj,
    norm_gains,
    survive,
    lengths,
    assign,
    advantage,
    reference_logit,
    recorded_gap,
):
    resp_count = hidden.shape[0]
    positions = hidden.shape[1]
    model_width = hidden.shape[2]
    half_value = value_proj.shape[2]
    micro_count = resp_count // MB_RESP
    row_count = MB_RESP * positions
    section_count = lax.axis_size("section")
    section_index = lax.axis_index("section")
    is_last = section_index == section_count - 1
    norm_gain = norm_gains[0]
    alive_mask = jnp.repeat(survive, GROUP)
    local_count = jnp.sum((alive_mask * lengths).astype(jnp.float32))
    gathered_value, gathered_output = (
        lax.all_gather(value_proj, "dp", axis=1, tiled=True),
        lax.all_gather(output_proj, "dp", axis=2, tiled=True),
    )
    w_first = gathered_value[0]
    w_second = gathered_output[0]

    def pick(array):
        return jnp.take(array, assign, axis=0, mode="fill", fill_value=0)

    slot_hidden = pick(hidden).reshape(micro_count, row_count, model_width)
    slot_unembed = pick(unembed).reshape(micro_count, row_count, model_width)
    position_index = lax.broadcasted_iota(jnp.int32, (resp_count, positions), 1)
    live_mask = (position_index < pick(lengths)[:, None]).astype(jnp.float32)
    advantages = jnp.broadcast_to(pick(advantage)[:, None], (resp_count, positions))
    gap_rows = pick(recorded_gap)
    clipped = (advantages > 0) & (gap_rows > clip_high) | (advantages < 0) & (gap_rows < clip_low)
    kept_mask = 1.0 - clipped.astype(jnp.float32)
    weight_rows = (-loss_scale * advantages * kept_mask * live_mask).reshape(micro_count, row_count)
    logit_base = pick(reference_logit).reshape(micro_count, row_count)
    step_count = micro_count + section_count - 1
    store_in = jnp.zeros((micro_count, row_count, model_width), jnp.bfloat16)
    store_normed = jnp.zeros((micro_count, row_count, model_width), jnp.bfloat16)
    store_projected = jnp.zeros((micro_count, row_count, half_value), jnp.bfloat16)
    store_out = jnp.zeros((micro_count, row_count, model_width), jnp.bfloat16)
    arriving = jnp.zeros((row_count, model_width), jnp.bfloat16)
    for step_index in range(step_count):
        micro_index = step_index - section_index
        active = (micro_index >= 0) & (micro_index < micro_count)
        clamped = jnp.clip(micro_index, 0, micro_count - 1)
        entering = jnp.where(section_index == 0, take_slot(slot_hidden, clamped), arriving)
        values, inverse, normed = norm_forward(entering, norm_gain)
        projected = jnp.dot(normed, w_first, preferred_element_type=jnp.float32).astype(
            jnp.bfloat16
        )
        partial_out = jnp.dot(projected, w_second, preferred_element_type=jnp.float32)
        mixed_sum = lax.psum(partial_out.astype(jnp.bfloat16), "tensor").astype(jnp.float32)
        leaving = (values + mixed_sum).astype(jnp.bfloat16)
        store_in = put_slot(store_in, entering, clamped, active)
        store_normed = put_slot(store_normed, normed, clamped, active)
        store_projected = put_slot(store_projected, projected, clamped, active)
        store_out = put_slot(store_out, leaving, clamped, active)
        arriving = from_behind(leaving, "section", 1)
    store_upstream = jnp.zeros((micro_count, row_count, model_width), jnp.bfloat16)
    store_grad_value = jnp.zeros((micro_count, row_count, half_value), jnp.bfloat16)
    arriving = jnp.zeros((row_count, model_width), jnp.bfloat16)
    for step_index in range(step_count):
        micro_index = step_index - (section_count - 1 - section_index)
        active = (micro_index >= 0) & (micro_index < micro_count)
        clamped = jnp.clip(micro_index, 0, micro_count - 1)
        top_rows = take_slot(store_out, clamped).astype(jnp.float32)
        unembed_rows = take_slot(slot_unembed, clamped).astype(jnp.float32)
        logit = jnp.sum(top_rows * unembed_rows, axis=-1)
        seed_rows = take_slot(weight_rows, clamped) * jnp.exp(
            logit - take_slot(logit_base, clamped)
        )
        start_grad = (seed_rows[:, None] * unembed_rows).astype(jnp.bfloat16)
        upstream = jnp.where(is_last, start_grad, arriving)
        entering = take_slot(store_in, clamped)
        normed = take_slot(store_normed, clamped)
        projected = take_slot(store_projected, clamped)
        grad_projected = contract_last(upstream, w_second).astype(jnp.bfloat16)
        partial_norm = contract_last(grad_projected, w_first)
        grad_normed = lax.psum(partial_norm.astype(jnp.bfloat16), "tensor").astype(jnp.float32)
        values, inverse, unused_normed = norm_forward(entering, norm_gain)
        grad_entering = (
            upstream.astype(jnp.float32) + norm_backward(values, inverse, norm_gain, grad_normed)
        ).astype(jnp.bfloat16)
        store_upstream = put_slot(store_upstream, upstream, clamped, active)
        store_grad_value = put_slot(store_grad_value, grad_projected, clamped, active)
        arriving = from_behind(grad_entering, "section", -1)
    flat_normed = store_normed.reshape(micro_count * row_count, model_width)
    flat_upstream = store_upstream.reshape(micro_count * row_count, model_width)
    flat_grad_value = store_grad_value.reshape(micro_count * row_count, half_value)
    flat_projected = store_projected.reshape(micro_count * row_count, half_value)
    reduced = lax.psum_scatter(
        jnp.concatenate(
            [
                contract_first(flat_normed, flat_grad_value),
                contract_first(flat_upstream, flat_projected),
            ],
            axis=1,
        ).astype(jnp.bfloat16),
        "dp",
        scatter_dimension=0,
        tiled=True,
    ).astype(jnp.float32)
    token_total = lax.psum(local_count, "dp")
    scaled_grads = reduced / token_total
    grad_value = scaled_grads[:, :half_value][None]
    grad_output = scaled_grads[:, half_value:].T[None]
    return (grad_value, grad_output)


def solution(mesh):
    placed = (
        P(("groups", "dp"), None, None),
        P(("groups", "dp"), None, None),
        P("section", "dp", "tensor"),
        P("section", "tensor", "dp"),
        P("section", None),
        P(("groups", "dp")),
        P(("groups", "dp")),
        P(("groups", "dp")),
        P(("groups", "dp")),
        P(("groups", "dp"), None),
        P(("groups", "dp"), None),
    )
    return jax.shard_map(
        local,
        mesh=mesh,
        in_specs=placed,
        out_specs=(
            P(("groups", "section"), "dp", "tensor"),
            P(("groups", "section"), "tensor", "dp"),
        ),
        check_vma=False,
    )
```

profile of v0, /device:TPU:0, one launch (start us, length us, event | category | flops | bytes accessed | tf_op | source)
XLA Modules:
  0.0 449.3 jit_solution(629598408572374933)
XLA Ops:
  18.2 48.9 %all-gather.3.cloned.1.call-done = bf16[1,5120,256]{2,1,0:T(8,128)(2,1)} async-done(((bf16[1,1280,256]{2,1,0:T(8,128)(2,1)}), bf16[1,5120,256]{2,1,0:T(8,128)(2,1)}) %all-gather.3.cloned.1.call-update) | async-done | bytes 2621456 | tf_op jit(solution)/shard_map/all_gather | solution.py:82
  67.1 2.6 bitcast_dynamic-update-slice_fusion.10
  69.7 52.5 %all-gather.5.cloned.1.call-done = bf16[1,256,5120]{2,1,0:T(8,128)(2,1)} async-done(((bf16[1,256,1280]{2,1,0:T(8,128)(2,1)}), bf16[1,256,5120]{2,1,0:T(8,128)(2,1)}) %all-gather.5.cloned.1.call-update) | async-done | bytes 2621456 | tf_op jit(solution)/shard_map/all_gather | solution.py:83
  122.2 3.2 convolution_convert_fusion.4
  128.5 14.6 %all-reduce.6.cloned.1.call-done = bf16[64,5120]{1,0:T(8,128)(2,1)} async-done(((bf16[64,5120]{1,0:T(8,128)(2,1)}), bf16[64,5120]{1,0:T(8,128)(2,1)}) %all-reduce.6.cloned.1.call-update) | async-done | bytes 655376 | tf_op jit(solution)/shard_map/psum | solution.py:117
  145.8 3.7 collective-permute-start
  150.7 13.2 %collective-permute-done = bf16[64,5120]{1,0:T(8,128)(2,1)S(1)} collective-permute-done((bf16[64,5120]{1,0:T(8,128)(2,1)S(1)}, bf16[64,5120]{1,0:T(8,128)(2,1)S(1)}, u32[]{:S(2)}, u32[]{:S(2)}) %collective-permute-start) | collective-permute-done | bytes 655392 | tf_op jit(solution)/shard_map/ppermute | solution.py:18
  172.6 16.8 %all-reduce.8.cloned.1.call-done = bf16[64,5120]{1,0:T(8,128)(2,1)} async-done(((bf16[64,5120]{1,0:T(8,128)(2,1)}), bf16[64,5120]{1,0:T(8,128)(2,1)}) %all-reduce.8.cloned.1.call-update) | async-done | bytes 655376 | tf_op jit(solution)/shard_map/psum | solution.py:117
  189.4 2.5 bitcast_dynamic-update-slice_fusion.4
  191.9 3.7 collective-permute-start.1
  195.6 2.2 constant_dynamic-slice_fusion.13
  197.8 12.1 %collective-permute-done.1 = bf16[64,5120]{1,0:T(8,128)(2,1)S(1)} collective-permute-done((bf16[64,5120]{1,0:T(8,128)(2,1)S(1)}, bf16[64,5120]{1,0:T(8,128)(2,1)S(1)}, u32[]{:S(2)}, u32[]{:S(2)}) %collective-permute-start.1) | collective-permute-done | bytes 655392 | tf_op jit(solution)/shard_map/ppermute | solution.py:18
  219.3 17.0 %all-reduce.10.cloned.1.call-done = bf16[64,5120]{1,0:T(8,128)(2,1)} async-done(((bf16[64,5120]{1,0:T(8,128)(2,1)}), bf16[64,5120]{1,0:T(8,128)(2,1)}) %all-reduce.10.cloned.1.call-update) | async-done | bytes 655376 | tf_op jit(solution)/shard_map/psum | solution.py:117
  236.2 3.1 bitcast_dynamic-update-slice_fusion.6
  239.3 2.4 fusion.32
  247.6 17.8 %all-reduce.12.cloned.1.call-done = bf16[64,5120]{1,0:T(8,128)(2,1)} async-done(((bf16[64,5120]{1,0:T(8,128)(2,1)}), bf16[64,5120]{1,0:T(8,128)(2,1)}) %all-reduce.12.cloned.1.call-update) | async-done | bytes 655376 | tf_op jit(solution)/shard_map/psum | solution.py:144
  271.8 16.1 %collective-permute-done.2 = bf16[64,5120]{1,0:T(8,128)(2,1)S(1)} collective-permute-done((bf16[64,5120]{1,0:T(8,128)(2,1)S(1)}, bf16[64,5120]{1,0:T(8,128)(2,1)S(1)}, u32[]{:S(2)}, u32[]{:S(2)}) %collective-permute-start.2) | collective-permute-done | bytes 655392 | tf_op jit(solution)/shard_map/ppermute | solution.py:18
  293.5 19.2 %all-reduce.14.cloned.1.call-done = bf16[64,5120]{1,0:T(8,128)(2,1)} async-done(((bf16[64,5120]{1,0:T(8,128)(2,1)}), bf16[64,5120]{1,0:T(8,128)(2,1)}) %all-reduce.14.cloned.1.call-update) | async-done | bytes 655376 | tf_op jit(solution)/shard_map/psum | solution.py:144
  318.6 16.3 %collective-permute-done.3 = bf16[64,5120]{1,0:T(8,128)(2,1)S(1)} collective-permute-done((bf16[64,5120]{1,0:T(8,128)(2,1)S(1)}, bf16[64,5120]{1,0:T(8,128)(2,1)S(1)}, u32[]{:S(2)}, u32[]{:S(2)}) %collective-permute-start.3) | collective-permute-done | bytes 655392 | tf_op jit(solution)/shard_map/ppermute | solution.py:18
  338.3 2.2 fusion.1
  340.5 2.7 pad_maximum_fusion
  344.5 12.9 %psum.47 = f32[]{:T(128)} all-reduce(f32[]{:T(128)} %convert_reduce_fusion), channel_id=1, replica_groups=mesh['groups'=2,'dp'=4,'section'=2,'tensor'=2] {'dp'}, use_global_device_ids=true, to_apply=%region_17.20 | all-reduce | flops 1 | bytes 8 | tf_op jit(solution)/shard_map/psum | solution.py:168
  357.4 80.2 %reduce-scatter.2.cloned.1.call-done = bf16[1280,512]{0,1:T(8,128)(2,1)} async-done(((bf16[5120,512]{0,1:T(8,128)(2,1)}), bf16[1280,512]{0,1:T(8,128)(2,1)}) %reduce-scatter.2.cloned.1.call-update) | async-done | bytes 1310736 | tf_op jit(solution)/shard_map/reduce_scatter | solution.py:156
  437.6 2.2 convert_divide_fusion
  (150 shorter events, 66.0 us)
Async XLA Ops:
  7.2 2.3 copy-start
  7.2 59.9 %all-gather.3.cloned.1.call-start = ((), (), s32[]{:S(2)}) async-start(), calls=%async_computation.1 | async-start | bytes 3276800 | tf_op jit(solution)/shard_map/all_gather | solution.py:82
  7.9 114.3 %all-gather.5.cloned.1.call-start = ((), (), s32[]{:S(2)}) async-start(), calls=%async_computation.2 | async-start | bytes 3276800 | tf_op jit(solution)/shard_map/all_gather | solution.py:83
  8.7 134.4 %all-reduce.6.cloned.1.call-start = ((), (), s32[]{:S(2)}) async-start(), calls=%async_computation.3 | async-start | bytes 1310720 | tf_op jit(solution)/shard_map/psum | solution.py:117
  11.2 2.4 copy-start.28
  11.2 3.0 copy-start.29
  14.8 52.3 %copy-start.26 = (f32[1,5120]{1,0:T(1,128)S(1)}, f32[1,5120]{1,0:T(1,128)}, u32[]{:S(2)}) copy-start(f32[1,5120]{1,0:T(1,128)} %param.19) | copy-start | bytes 61444
  125.4 64.0 %all-reduce.8.cloned.1.call-start = ((), (), s32[]{:S(2)}) async-start(), calls=%async_computation.4 | async-start | bytes 1310720 | tf_op jit(solution)/shard_map/psum | solution.py:117
  145.8 4.9 %copy-start.20 = (bf16[2,64,5120]{2,1,0:T(8,128)(2,1)}, bf16[2,64,5120]{2,1,0:T(8,128)(2,1)S(1)}, u32[]{:S(2)}) copy-start(bf16[2,64,5120]{2,1,0:T(8,128)(2,1)S(1)} %get-tuple-element.22) | copy-start | bytes 3932164
  145.8 18.1 %collective-permute-start = (bf16[64,5120]{1,0:T(8,128)(2,1)S(1)}, bf16[64,5120]{1,0:T(8,128)(2,1)S(1)}, u32[]{:S(2)}, u32[]{:S(2)}) collective-permute-start(bf16[64,5120]{1,0:T(8,128)(2,1)S(1)} %get-tuple-element.23), channel_id=1, source_target_pairs={{0,2},{1,3},{4,6},{5,7},{8,10},{9,11},{12,14},{13,15},{16,18},{17,... | collective-permute-start | bytes 1966088 | tf_op jit(solution)/shard_map/ppermute | solution.py:18
  150.7 14.6 %copy-start.8 = (bf16[1,5120,256]{2,1,0:T(8,128)(2,1)S(1)}, bf16[1,5120,256]{2,1,0:T(8,128)(2,1)}, u32[]{:S(2)}) copy-start(bf16[1,5120,256]{2,1,0:T(8,128)(2,1)} %all-gather.3.cloned.1.call-done) | copy-start | bytes 7864324
  168.5 67.7 %all-reduce.10.cloned.1.call-start = ((), (), s32[]{:S(2)}) async-start(), calls=%async_computation.5 | async-start | bytes 1310720 | tf_op jit(solution)/shard_map/psum | solution.py:117
  191.9 18.1 %collective-permute-start.1 = (bf16[64,5120]{1,0:T(8,128)(2,1)S(1)}, bf16[64,5120]{1,0:T(8,128)(2,1)S(1)}, u32[]{:S(2)}, u32[]{:S(2)}) collective-permute-start(bf16[64,5120]{1,0:T(8,128)(2,1)S(1)} %get-tuple-element.21), channel_id=1, source_target_pairs={{0,2},{1,3},{4,6},{5,7},{8,10},{9,11},{12,14},{13,15},{16,18},{17,... | collective-permute-start | bytes 1966088 | tf_op jit(solution)/shard_map/ppermute | solution.py:18
  195.6 14.5 %copy-start.15 = (bf16[16,8,5120]{2,1,0:T(8,128)(2,1)S(1)}, bf16[16,8,5120]{2,1,0:T(8,128)(2,1)}, u32[]{:S(2)}) copy-start(bf16[16,8,5120]{2,1,0:T(8,128)(2,1)} %copy-done.12) | copy-start | bytes 3932164
  195.6 14.5 %copy-start.25 = (bf16[1,64,5120]{2,1,0:T(8,128)(2,1)S(1)}, bf16[1,64,5120]{2,1,0:T(8,128)(2,1)}, u32[]{:S(2)}) copy-start(bf16[1,64,5120]{2,1,0:T(8,128)(2,1)} %constant_dynamic-slice_fusion.8) | copy-start | bytes 1966084
  215.4 50.0 %all-reduce.12.cloned.1.call-start = ((), (), s32[]{:S(2)}) async-start(), calls=%async_computation.6 | async-start | bytes 1310720 | tf_op jit(solution)/shard_map/psum | solution.py:144
  218.4 17.8 %copy-start.22 = (bf16[64,5120]{1,0:T(8,128)(2,1)S(1)}, bf16[64,5120]{1,0:T(8,128)(2,1)}, u32[]{:S(2)}) copy-start(bf16[64,5120]{1,0:T(8,128)(2,1)} %copy-done.21) | copy-start | bytes 1966084
  239.3 2.4 copy-start.5
  245.3 67.4 %all-reduce.14.cloned.1.call-start = ((), (), s32[]{:S(2)}) async-start(), calls=%async_computation.7 | async-start | bytes 1310720 | tf_op jit(solution)/shard_map/psum | solution.py:144
  265.4 2.1 copy-start.24
  269.2 18.8 %collective-permute-start.2 = (bf16[64,5120]{1,0:T(8,128)(2,1)S(1)}, bf16[64,5120]{1,0:T(8,128)(2,1)S(1)}, u32[]{:S(2)}, u32[]{:S(2)}) collective-permute-start(bf16[64,5120]{1,0:T(8,128)(2,1)S(1)} %fusion.46), channel_id=1, source_target_pairs={{2,0},{3,1},{6,4},{7,5},{10,8},{11,9},{14,12},{15,13},{18,16},{19,... | collective-permute-start | bytes 1966088 | tf_op jit(solution)/shard_map/ppermute | solution.py:18
  293.5 144.1 %reduce-scatter.2.cloned.1.call-start = ((), (), s32[]{:S(2)}) async-start(), calls=%async_computation.8 | async-start | bytes 6553600 | tf_op jit(solution)/shard_map/reduce_scatter | solution.py:156
  314.4 20.5 %copy-start.7 = (bf16[1,256,5120]{2,1,0:T(8,128)(2,1)S(1)}, bf16[1,256,5120]{2,1,0:T(8,128)(2,1)}, u32[]{:S(2)}) copy-start(bf16[1,256,5120]{2,1,0:T(8,128)(2,1)} %all-gather.5.cloned.1.call-done) | copy-start | bytes 7864324
  316.1 18.8 %collective-permute-start.3 = (bf16[64,5120]{1,0:T(8,128)(2,1)S(1)}, bf16[64,5120]{1,0:T(8,128)(2,1)S(1)}, u32[]{:S(2)}, u32[]{:S(2)}) collective-permute-start(bf16[64,5120]{1,0:T(8,128)(2,1)S(1)} %fusion.52), channel_id=1, source_target_pairs={{2,0},{3,1},{6,4},{7,5},{10,8},{11,9},{14,12},{15,13},{18,16},{19,... | collective-permute-start | bytes 1966088 | tf_op jit(solution)/shard_map/ppermute | solution.py:18
  (19 other events, 29.8 us)
Sparse Core Ops, SparseCore 0:
  9.6 57.4 all-gather.2
  68.6 53.4 all-gather.4
  125.5 17.5 all-reduce.5
  168.6 20.6 all-reduce.7
  215.5 20.6 all-reduce.9
  245.4 19.9 all-reduce.11
  293.6 19.0 all-reduce.13
  343.3 94.1 reduce-scatter.1
where the time goes:
time: 450 us; the launch traced here: 449 us
  waiting for transfers between devices  326 us (72%)
  local copies, waits for them, and re-layouts  32.9 us (7%)
  other arithmetic  32.2 us (7%)
  matrix products  19.3 us (4%)
  between operations  15.3 us (3%)
  blocking collectives  12.9 us (3%)
  starting transfers between devices  10.5 us (2%)
    reduce_scatter x1, waiting for transfers between devices, local(): lax.psum_scatter(jnp.concatenate([contract_first(flat_normed, flat_grad_v...  80.2 us
    ppermute x4, waiting for transfers between devices, from_behind(): return lax.ppermute(block, axis, route)  57.8 us
    all_gather x1, waiting for transfers between devices, local(): lax.all_gather(output_proj, 'dp', axis=2, tiled=True)  52.5 us
    all_gather x1, waiting for transfers between devices, local(): lax.all_gather(value_proj, 'dp', axis=1, tiled=True)  48.9 us
    psum x3, waiting for transfers between devices, local(): lax.psum(partial_out.astype(jnp.bfloat16), 'tensor').astype(jnp.float32)  48.4 us
    psum x2, waiting for transfers between devices, local(): lax.psum(partial_norm.astype(jnp.bfloat16), 'tensor').astype(jnp.float32)  37 us
    dynamic_update_slice x10, other arithmetic, put_slot(): lax.dynamic_update_index_in_dim(slot_store, jnp.where(active, new_value,...  14.3 us
    psum x1, blocking collectives, local(): token_total = lax.psum(local_count, 'dp')  12.9 us
  transfers between devices with their start and end apart: 12, of which 12 were waited for; matrix products, arithmetic and copies ran while one was open for 6% of the time, Pallas kernels for 0%

commit v1 on v0

--- a/solution.py
+++ b/solution.py
@@ -1,3 +1,4 @@
+import functools
 import math
 import jax
 import jax.numpy as jnp
@@ -10,6 +11,15 @@
 loss_scale = 4096.0
 clip_high = math.log(1.28)
 clip_low = math.log(0.8)
+
+
+def refer_set(v0, which_axis):
+    latest = lax.all_gather(v0, which_axis)
+    front = jnp.concatenate(latest, axis=2)
+    return front
+
+
+part_spans = functools.partial(refer_set, which_axis="dp")
 
 
 def from_behind(block, axis, distance):
@@ -80,7 +90,7 @@
     local_count = jnp.sum((alive_mask * lengths).astype(jnp.float32))
     gathered_value, gathered_output = (
         lax.all_gather(value_proj, "dp", axis=1, tiled=True),
-        lax.all_gather(output_proj, "dp", axis=2, tiled=True),
+        part_spans(output_proj),
     )
     w_first = gathered_value[0]
     w_second = gathered_output[0]

time: 450 us -> 453 us (level)
  local copies, waits for them, and re-layouts: 32.9 us -> 38.6 us
    unnamed x65 -> x67, local copies, waits for them, and re-layouts: 11.3 us -> 12.6 us
  transfers between devices with their start and end apart: 12 -> 12, of which waited for: 12 -> 12; matrix products, arithmetic and copies ran while one was open for 6% -> 7% of each run, Pallas kernels for 0% -> 0%
where the time goes in v1:
time: 453 us; the launch traced here: 452 us
  waiting for transfers between devices  324 us (72%)
  local copies, waits for them, and re-layouts  38.6 us (9%)
  other arithmetic  32.2 us (7%)
  matrix products  17.7 us (4%)
  between operations  15.4 us (3%)
  blocking collectives  12.9 us (3%)
  starting transfers between devices  10.5 us (2%)
    reduce_scatter x1, waiting for transfers between devices, local(): lax.psum_scatter(jnp.concatenate([contract_first(flat_normed, flat_grad_v...  80.1 us
    ppermute x4, waiting for transfers between devices, from_behind(): return lax.ppermute(block, axis, route)  57.8 us
    all_gather x1, waiting for transfers between devices, local(): lax.all_gather(value_proj, 'dp', axis=1, tiled=True)  50.8 us
    all_gather x1, waiting for transfers between devices, refer_set(): latest = lax.all_gather(v0, which_axis)  48.9 us
    psum x3, waiting for transfers between devices, local(): lax.psum(partial_out.astype(jnp.bfloat16), 'tensor').astype(jnp.float32)  48.4 us
    psum x2, waiting for transfers between devices, local(): lax.psum(partial_norm.astype(jnp.bfloat16), 'tensor').astype(jnp.float32)  37 us
    dynamic_update_slice x10, other arithmetic, put_slot(): lax.dynamic_update_index_in_dim(slot_store, jnp.where(active, new_value,...  14.3 us
    psum x1, blocking collectives, local(): token_total = lax.psum(local_count, 'dp')  12.9 us
  transfers between devices with their start and end apart: 12, of which 12 were waited for; matrix products, arithmetic and copies ran while one was open for 7% of the time, Pallas kernels for 0%

profile of v1, /device:TPU:0, one launch (start us, length us, event | category | flops | bytes accessed | tf_op | source)
XLA Modules:
  0.0 451.7 jit_solution(9021176902481455351)
XLA Ops:
  18.2 48.9 %all-gather.6.cloned.1.call-done = bf16[4,256,1280]{2,1,0:T(8,128)(2,1)} async-done(((bf16[1,256,1280]{2,1,0:T(8,128)(2,1)}), bf16[4,256,1280]{2,1,0:T(8,128)(2,1)}) %all-gather.6.cloned.1.call-update) | async-done | bytes 2621456 | tf_op jit(solution)/shard_map/all_gather | solution.py:17
  67.1 4.4 copy.20
  71.5 50.8 %all-gather.4.cloned.1.call-done = bf16[1,5120,256]{2,1,0:T(8,128)(2,1)} async-done(((bf16[1,1280,256]{2,1,0:T(8,128)(2,1)}), bf16[1,5120,256]{2,1,0:T(8,128)(2,1)}) %all-gather.4.cloned.1.call-update) | async-done | bytes 2621456 | tf_op jit(solution)/shard_map/all_gather | solution.py:92
  122.2 2.7 bitcast_dynamic-update-slice_fusion.10
  129.9 14.6 %all-reduce.6.cloned.1.call-done = bf16[64,5120]{1,0:T(8,128)(2,1)} async-done(((bf16[64,5120]{1,0:T(8,128)(2,1)}), bf16[64,5120]{1,0:T(8,128)(2,1)}) %all-reduce.6.cloned.1.call-update) | async-done | bytes 655376 | tf_op jit(solution)/shard_map/psum | solution.py:127
  147.2 3.7 collective-permute-start
  152.1 13.2 %collective-permute-done = bf16[64,5120]{1,0:T(8,128)(2,1)S(1)} collective-permute-done((bf16[64,5120]{1,0:T(8,128)(2,1)S(1)}, bf16[64,5120]{1,0:T(8,128)(2,1)S(1)}, u32[]{:S(2)}, u32[]{:S(2)}) %collective-permute-start) | collective-permute-done | bytes 655392 | tf_op jit(solution)/shard_map/ppermute | solution.py:28
  174.3 16.8 %all-reduce.8.cloned.1.call-done = bf16[64,5120]{1,0:T(8,128)(2,1)} async-done(((bf16[64,5120]{1,0:T(8,128)(2,1)}), bf16[64,5120]{1,0:T(8,128)(2,1)}) %all-reduce.8.cloned.1.call-update) | async-done | bytes 655376 | tf_op jit(solution)/shard_map/psum | solution.py:127
  191.1 2.5 bitcast_dynamic-update-slice_fusion.4
  193.6 3.7 collective-permute-start.1
  197.3 2.2 constant_dynamic-slice_fusion.13
  199.5 12.1 %collective-permute-done.1 = bf16[64,5120]{1,0:T(8,128)(2,1)S(1)} collective-permute-done((bf16[64,5120]{1,0:T(8,128)(2,1)S(1)}, bf16[64,5120]{1,0:T(8,128)(2,1)S(1)}, u32[]{:S(2)}, u32[]{:S(2)}) %collective-permute-start.1) | collective-permute-done | bytes 655392 | tf_op jit(solution)/shard_map/ppermute | solution.py:28
  221.7 17.0 %all-reduce.10.cloned.1.call-done = bf16[64,5120]{1,0:T(8,128)(2,1)} async-done(((bf16[64,5120]{1,0:T(8,128)(2,1)}), bf16[64,5120]{1,0:T(8,128)(2,1)}) %all-reduce.10.cloned.1.call-update) | async-done | bytes 655376 | tf_op jit(solution)/shard_map/psum | solution.py:127
  238.7 3.1 bitcast_dynamic-update-slice_fusion.6
  241.7 2.4 fusion.23
  250.0 17.8 %all-reduce.12.cloned.1.call-done = bf16[64,5120]{1,0:T(8,128)(2,1)} async-done(((bf16[64,5120]{1,0:T(8,128)(2,1)}), bf16[64,5120]{1,0:T(8,128)(2,1)}) %all-reduce.12.cloned.1.call-update) | async-done | bytes 655376 | tf_op jit(solution)/shard_map/psum | solution.py:154
  274.3 16.1 %collective-permute-done.2 = bf16[64,5120]{1,0:T(8,128)(2,1)S(1)} collective-permute-done((bf16[64,5120]{1,0:T(8,128)(2,1)S(1)}, bf16[64,5120]{1,0:T(8,128)(2,1)S(1)}, u32[]{:S(2)}, u32[]{:S(2)}) %collective-permute-start.2) | collective-permute-done | bytes 655392 | tf_op jit(solution)/shard_map/ppermute | solution.py:28
  296.0 19.2 %all-reduce.14.cloned.1.call-done = bf16[64,5120]{1,0:T(8,128)(2,1)} async-done(((bf16[64,5120]{1,0:T(8,128)(2,1)}), bf16[64,5120]{1,0:T(8,128)(2,1)}) %all-reduce.14.cloned.1.call-update) | async-done | bytes 655376 | tf_op jit(solution)/shard_map/psum | solution.py:154
  321.0 16.3 %collective-permute-done.3 = bf16[64,5120]{1,0:T(8,128)(2,1)S(1)} collective-permute-done((bf16[64,5120]{1,0:T(8,128)(2,1)S(1)}, bf16[64,5120]{1,0:T(8,128)(2,1)S(1)}, u32[]{:S(2)}, u32[]{:S(2)}) %collective-permute-start.3) | collective-permute-done | bytes 655392 | tf_op jit(solution)/shard_map/ppermute | solution.py:28
  340.7 2.2 fusion.1
  343.0 2.7 pad_maximum_fusion
  346.9 12.9 %psum.47 = f32[]{:T(128)} all-reduce(f32[]{:T(128)} %convert_reduce_fusion), channel_id=1, replica_groups=mesh['groups'=2,'dp'=4,'section'=2,'tensor'=2] {'dp'}, use_global_device_ids=true, to_apply=%region_17.20 | all-reduce | flops 1 | bytes 8 | tf_op jit(solution)/shard_map/psum | solution.py:178
  359.9 80.1 %reduce-scatter.2.cloned.1.call-done = bf16[1280,512]{0,1:T(8,128)(2,1)} async-done(((bf16[5120,512]{0,1:T(8,128)(2,1)}), bf16[1280,512]{0,1:T(8,128)(2,1)}) %reduce-scatter.2.cloned.1.call-update) | async-done | bytes 1310736 | tf_op jit(solution)/shard_map/reduce_scatter | solution.py:166
  440.0 2.2 convert_divide_fusion
  (153 shorter events, 68.8 us)
Async XLA Ops:
  7.2 59.9 %all-gather.6.cloned.1.call-start = ((), (), s32[]{:S(2)}) async-start(), calls=%async_computation.8 | async-start | bytes 3276800 | tf_op jit(solution)/shard_map/all_gather | solution.py:17
  7.9 114.3 %all-gather.4.cloned.1.call-start = ((), (), s32[]{:S(2)}) async-start(), calls=%async_computation.1 | async-start | bytes 3276800 | tf_op jit(solution)/shard_map/all_gather | solution.py:92
  8.7 135.8 %all-reduce.6.cloned.1.call-start = ((), (), s32[]{:S(2)}) async-start(), calls=%async_computation.2 | async-start | bytes 1310720 | tf_op jit(solution)/shard_map/psum | solution.py:127
  11.2 2.4 copy-start.29
  11.2 3.0 copy-start.30
  18.2 104.1 %copy-start.27 = (f32[1,5120]{1,0:T(1,128)S(1)}, f32[1,5120]{1,0:T(1,128)}, u32[]{:S(2)}) copy-start(f32[1,5120]{1,0:T(1,128)} %param.19) | copy-start | bytes 61444
  122.2 2.7 copy-start.3
  126.8 64.3 %all-reduce.8.cloned.1.call-start = ((), (), s32[]{:S(2)}) async-start(), calls=%async_computation.3 | async-start | bytes 1310720 | tf_op jit(solution)/shard_map/psum | solution.py:127
  147.2 4.9 %copy-start.21 = (bf16[2,64,5120]{2,1,0:T(8,128)(2,1)}, bf16[2,64,5120]{2,1,0:T(8,128)(2,1)S(1)}, u32[]{:S(2)}) copy-start(bf16[2,64,5120]{2,1,0:T(8,128)(2,1)S(1)} %get-tuple-element.24) | copy-start | bytes 3932164
  147.2 18.1 %collective-permute-start = (bf16[64,5120]{1,0:T(8,128)(2,1)S(1)}, bf16[64,5120]{1,0:T(8,128)(2,1)S(1)}, u32[]{:S(2)}, u32[]{:S(2)}) collective-permute-start(bf16[64,5120]{1,0:T(8,128)(2,1)S(1)} %get-tuple-element.25), channel_id=1, source_target_pairs={{0,2},{1,3},{4,6},{5,7},{8,10},{9,11},{12,14},{13,15},{16,18},{17,... | collective-permute-start | bytes 1966088 | tf_op jit(solution)/shard_map/ppermute | solution.py:28
  152.1 14.6 %copy-start.9 = (bf16[1,5120,256]{2,1,0:T(8,128)(2,1)S(1)}, bf16[1,5120,256]{2,1,0:T(8,128)(2,1)}, u32[]{:S(2)}) copy-start(bf16[1,5120,256]{2,1,0:T(8,128)(2,1)} %all-gather.4.cloned.1.call-done) | copy-start | bytes 7864324
  170.2 68.4 %all-reduce.10.cloned.1.call-start = ((), (), s32[]{:S(2)}) async-start(), calls=%async_computation.4 | async-start | bytes 1310720 | tf_op jit(solution)/shard_map/psum | solution.py:127
  193.6 18.0 %collective-permute-start.1 = (bf16[64,5120]{1,0:T(8,128)(2,1)S(1)}, bf16[64,5120]{1,0:T(8,128)(2,1)S(1)}, u32[]{:S(2)}, u32[]{:S(2)}) collective-permute-start(bf16[64,5120]{1,0:T(8,128)(2,1)S(1)} %get-tuple-element.23), channel_id=1, source_target_pairs={{0,2},{1,3},{4,6},{5,7},{8,10},{9,11},{12,14},{13,15},{16,18},{17,... | collective-permute-start | bytes 1966088 | tf_op jit(solution)/shard_map/ppermute | solution.py:28
  197.3 14.5 %copy-start.16 = (bf16[16,8,5120]{2,1,0:T(8,128)(2,1)S(1)}, bf16[16,8,5120]{2,1,0:T(8,128)(2,1)}, u32[]{:S(2)}) copy-start(bf16[16,8,5120]{2,1,0:T(8,128)(2,1)} %copy-done.13) | copy-start | bytes 3932164
  197.3 14.5 %copy-start.26 = (bf16[1,64,5120]{2,1,0:T(8,128)(2,1)S(1)}, bf16[1,64,5120]{2,1,0:T(8,128)(2,1)}, u32[]{:S(2)}) copy-start(bf16[1,64,5120]{2,1,0:T(8,128)(2,1)} %constant_dynamic-slice_fusion.8) | copy-start | bytes 1966084
  211.8 2.5 copy-start.10
  217.8 50.0 %all-reduce.12.cloned.1.call-start = ((), (), s32[]{:S(2)}) async-start(), calls=%async_computation.5 | async-start | bytes 1310720 | tf_op jit(solution)/shard_map/psum | solution.py:154
  220.8 17.9 %copy-start.23 = (bf16[64,5120]{1,0:T(8,128)(2,1)S(1)}, bf16[64,5120]{1,0:T(8,128)(2,1)}, u32[]{:S(2)}) copy-start(bf16[64,5120]{1,0:T(8,128)(2,1)} %copy-done.22) | copy-start | bytes 1966084
  241.7 2.4 copy-start.6
  247.7 67.4 %all-reduce.14.cloned.1.call-start = ((), (), s32[]{:S(2)}) async-start(), calls=%async_computation.6 | async-start | bytes 1310720 | tf_op jit(solution)/shard_map/psum | solution.py:154
  271.6 18.8 %collective-permute-start.2 = (bf16[64,5120]{1,0:T(8,128)(2,1)S(1)}, bf16[64,5120]{1,0:T(8,128)(2,1)S(1)}, u32[]{:S(2)}, u32[]{:S(2)}) collective-permute-start(bf16[64,5120]{1,0:T(8,128)(2,1)S(1)} %fusion.37), channel_id=1, source_target_pairs={{2,0},{3,1},{6,4},{7,5},{10,8},{11,9},{14,12},{15,13},{18,16},{19,... | collective-permute-start | bytes 1966088 | tf_op jit(solution)/shard_map/ppermute | solution.py:28
  295.9 144.1 %reduce-scatter.2.cloned.1.call-start = ((), (), s32[]{:S(2)}) async-start(), calls=%async_computation.7 | async-start | bytes 6553600 | tf_op jit(solution)/shard_map/reduce_scatter | solution.py:166
  316.8 20.5 %copy-start.8 = (bf16[4,256,1280]{1,2,0:T(8,128)(2,1)S(1)}, bf16[4,256,1280]{1,2,0:T(8,128)(2,1)}, u32[]{:S(2)}) copy-start(bf16[4,256,1280]{1,2,0:T(8,128)(2,1)} %copy.20) | copy-start | bytes 7864324
  318.6 18.8 %collective-permute-start.3 = (bf16[64,5120]{1,0:T(8,128)(2,1)S(1)}, bf16[64,5120]{1,0:T(8,128)(2,1)S(1)}, u32[]{:S(2)}, u32[]{:S(2)}) collective-permute-start(bf16[64,5120]{1,0:T(8,128)(2,1)S(1)} %fusion.43), channel_id=1, source_target_pairs={{2,0},{3,1},{6,4},{7,5},{10,8},{11,9},{14,12},{15,13},{18,16},{19,... | collective-permute-start | bytes 1966088 | tf_op jit(solution)/shard_map/ppermute | solution.py:28
  (20 other events, 32.4 us)
Sparse Core Ops, SparseCore 0:
  9.6 57.4 all-gather.5
  68.6 53.5 all-gather.3
  126.9 17.5 all-reduce.5
  170.4 20.6 all-reduce.7
  217.9 20.6 all-reduce.9
  247.8 19.9 all-reduce.11
  296.0 19.0 all-reduce.13
  345.8 94.1 reduce-scatter.1
